TPU v7x, 32 devices: a whole 2x2x4 slice. The times are simulated.
32 devices in a mesh: dp: 8 (over y, x, core), tp: 4 (over z).
Axes of the slice: x: 2, y: 2, z: 4, core: 2. Of those that a mesh axis runs over, the one named last changes fastest.
Arguments:
- inputs: bfloat16 [8, 768, 1280], P('dp', 'tp'), may hold values from -6 to 6
- saved_hidden: bfloat16 [8, 768, 5120], P('dp', None, 'tp'), may hold values from -8 to 8
- upstream: bfloat16 [8, 768, 1280], P('dp', 'tp'), may hold values from -6 to 6
- w_in: bfloat16 [1280, 5120], P(None, 'tp'), may hold values from -0.15625 to 0.15625
- w_out: bfloat16 [5120, 1280], P('tp'), may hold values from -0.078125 to 0.078125
- kernel: float32 [7, 1280], replicated, may hold values from -2 to 2
Outputs:
- grad_inputs: bfloat16 [8, 768, 1280], P('dp', 'tp')
- grad_w_in: float32 [1280, 5120], P(None, 'tp')
- grad_w_out: float32 [5120, 1280], P('tp')
- grad_bias: float32 [5120], P('tp')
- grad_kernel: float32 [7, 1280], replicated
All inputs are finite; a program needn't handle non-finite values.
Results may differ from a plain program's by a relative error of at most 0.02.
Values may be sent and summed in bfloat16 or wider, within the bound.
No kernel may reach another device: no remote copies, remote signals or barrier semaphores. Data moves between devices by JAX's collectives and lax.ppermute only.
A program may use at most 128 MiB of HBM per device.

v0:
```python
import jax
import jax.numpy as jnp
from jax import lax
from jax.sharding import PartitionSpec as P

KW = 7


def with_halo(cells, sides, width):
    for axis, dim in sides:
        count = lax.axis_size(axis)
        ends = count - 1
        head = lax.slice_in_dim(cells, 0, width, axis=dim)
        tail = lax.slice_in_dim(cells, cells.shape[dim] - width, cells.shape[dim], axis=dim)
        cells = jnp.concatenate(
            [
                lax.ppermute(tail, axis, [(i, (i + 1) % count) for i in range(ends)]),
                cells,
                lax.ppermute(head, axis, [((i + 1) % count, i) for i in range(ends)]),
            ],
            axis=dim,
        )
    return cells


def gelu_exact(value):
    return jax.nn.gelu(value, approximate=False)


def convolve(padded, kernel, length):
    mixed = padded[3 : 3 + length].astype(jnp.float32)
    for tap in range(KW):
        mixed = mixed + kernel[tap] * padded[tap : tap + length].astype(jnp.float32)
    return mixed.astype(jnp.bfloat16)


def shards(inputs, saved_hidden, upstream, w_in, w_out, kernel):
    tokens = inputs[0]
    hidden = saved_hidden[0]
    grad_out = upstream[0]
    length = tokens.shape[0]
    piece = lax.all_gather(grad_out, "tp", axis=0, tiled=True)
    hidden_rows = hidden.astype(jnp.float32)
    back_rows = lax.dot_general(
        piece, w_out, (((1,), (1,)), ((), ())), preferred_element_type=jnp.float32
    )
    grad_rows = jax.vjp(gelu_exact, hidden_rows)[1](back_rows)[0].astype(jnp.bfloat16)
    buffer = grad_rows
    activated = gelu_exact(hidden_rows).astype(jnp.bfloat16)
    total = lax.dot_general(
        activated, piece, (((0,), (0,)), ((), ())), preferred_element_type=jnp.float32
    )
    grad_w_out = total
    grad_bias = jnp.sum(buffer.astype(jnp.float32), axis=0)
    summed = lax.psum_scatter(
        lax.dot_general(
            buffer, w_in, (((1,), (1,)), ((), ())), preferred_element_type=jnp.float32
        ).astype(jnp.bfloat16),
        "tp",
        scatter_dimension=0,
        tiled=True,
    ).astype(jnp.float32)
    grad_mixed = (grad_out.astype(jnp.float32) + summed).astype(jnp.bfloat16)
    padded = with_halo(tokens, (("tp", 0),), 3)
    mixed = convolve(padded, kernel, length)
    grad_rows = buffer
    grad_w_in = lax.dot_general(
        lax.all_gather(mixed, "tp", axis=0, tiled=True),
        grad_rows,
        (((0,), (0,)), ((), ())),
        preferred_element_type=jnp.float32,
    )
    grad_pad = with_halo(grad_mixed, (("tp", 0),), 3)
    grad_f = grad_mixed.astype(jnp.float32)
    grad_inputs = grad_f
    taps = []
    for tap in range(KW):
        grad_inputs = grad_inputs + kernel[tap] * grad_pad[6 - tap : 6 - tap + length].astype(
            jnp.float32
        )
        taps.append(jnp.sum(grad_f * padded[tap : tap + length].astype(jnp.float32), axis=0))
    grad_kernel = jnp.stack(taps)
    grad_kernel = lax.psum(grad_kernel, ("dp", "tp"))
    grad_w_in, grad_w_out, grad_bias = (
        lax.psum(grad_w_in.astype(jnp.bfloat16), "dp").astype(jnp.float32),
        lax.psum(grad_w_out.astype(jnp.bfloat16), "dp").astype(jnp.float32),
        lax.psum(grad_bias.astype(jnp.bfloat16), "dp").astype(jnp.float32),
    )
    return (grad_inputs.astype(jnp.bfloat16)[None], grad_w_in, grad_w_out, grad_bias, grad_kernel)


def solution(mesh):
    in_specs = (
        P("dp", "tp", None),
        P("dp", None, "tp"),
        P("dp", "tp", None),
        P(None, "tp"),
        P("tp", None),
        P(),
    )
    out_specs = (P("dp", "tp", None), P(None, "tp"), P("tp", None), P("tp"), P())
    return jax.shard_map(shards, mesh=mesh, in_specs=in_specs, out_specs=out_specs, check_vma=False)
```

profile of v0, /device:TPU:0, one launch (start us, length us, event | category | flops | bytes accessed | tf_op | source)
XLA Modules:
  0.0 318.5 jit_solution(17866380397956469389)
XLA Ops:
  7.2 0.0 copy-start
  7.2 0.0 all-gather.6.cloned.1.call-start
  7.2 0.7 all-gather.6.cloned.1.call-update
  7.9 0.0 all-gather.4.cloned.1.call-start
  8.0 1.0 slice_bitcast_fusion.1
  8.9 5.0 %collective-permute-start.2 = (bf16[3,1280]{1,0:T(4,128)(2,1)S(1)}, bf16[3,1280]{1,0:T(4,128)(2,1)S(1)}, u32[]{:S(2)}, u32[]{:S(2)}) collective-permute-start(bf16[3,1280]{1,0:T(4,128)(2,1)S(1)} %get-tuple-element.27), channel_id=1, source_target_pairs={{0,1},{1,2},{2,3},{4,5},{5,6},{6,7},{8,9},{9,10},{10,11},{12,13},{... | collective-permute-start | bytes 23048 | tf_op jit(solution)/shard_map/ppermute | solution.py:17
  13.9 1.3 collective-permute-start.3
  15.2 1.3 slice_reduce_fusion.6
  16.4 0.0 collective-permute-done.2
  16.5 3.0 collective-permute-done.3
  19.4 4.4 %fusion.52 = bf16[192,1280]{1,0:T(8,128)(2,1)} fusion(bf16[192,1280]{1,0:T(8,128)(2,1)} %bitcast.131, bf16[3,1280]{1,0:T(4,128)(2,1)S(1)} %collective-permute-done.3, bf16[3,1280]{1,0:T(4,128)(2,1)S(1)} %collective-permute-done.2, f32[1280]{0:T(1024)S(1)} %get-tuple-element.20, f32[1280]{0:T(1024)S(1)} %get-tuple-element.21, f32[1280]{0:T(1024)S(1)} %get-tuple-element.16, ...), kind=kLoop, calls=%fused_computation.72 | loop fusion | flops 9830400 | bytes 1034240 | tf_op jit(solution)/shard_map/convert_element_type | solution.py:34
  23.8 0.0 all-gather.4.cloned.1.call-update
  23.9 0.0 all-reduce.3.cloned.1.call-start
  23.9 10.1 %fusion.38 = f32[768,1280]{1,0:T(8,128)} fusion(bf16[1,768,1280]{2,1,0:T(8,128)(2,1)} %param.7), kind=kLoop, calls=%fused_computation.43 | loop fusion | flops 61931520 | bytes 5898240 | tf_op jit(solution)/shard_map/jvp()/erfc | solution.py:27
  34.0 21.8 %all-gather.6.cloned.1.call-done = bf16[1,768,1280]{2,1,0:T(8,128)(2,1)} async-done(((bf16[1,192,1280]{2,1,0:T(8,128)(2,1)}), bf16[1,768,1280]{2,1,0:T(8,128)(2,1)}) %all-gather.6.cloned.1.call-update) | async-done | bytes 1966096 | tf_op jit(solution)/shard_map/all_gather | solution.py:42
  55.8 0.0 copy-start.1
  55.8 0.0 copy-start.4
  55.8 0.0 copy-start.5
  55.8 7.9 %convolution_convert_fusion = bf16[1280,1280]{1,0:T(8,128)(2,1)} fusion(f32[768,1280]{1,0:T(8,128)} %fusion.38, bf16[1,768,1280]{2,1,0:T(8,128)(2,1)} %param.7, bf16[1,768,1280]{2,1,0:T(8,128)(2,1)} %all-gather.6.cloned.1.call-done), kind=kOutput, calls=%fused_computation | convolution fusion | flops 2522152960 | bytes 11141120 | tf_op jit(solution)/shard_map/dot_general | solution.py:50
  63.7 0.0 copy-done
  63.7 0.0 copy-done.1
  63.7 0.0 copy-done.4
  63.7 0.0 copy-done.5
  63.8 4.7 %fusion.80 = (bf16[1280]{0:T(1024)(128)(2,1)S(1)}, bf16[768,1280]{1,0:T(8,128)(2,1)}) fusion(f32[768,1280]{1,0:T(8,128)S(1)} %copy-done.1, bf16[1280,1280]{1,0:T(8,128)(2,1)S(1)} %copy-done, bf16[1,768,1280]{2,1,0:T(8,128)(2,1)S(1)} %copy-done.5, bf16[1,768,1280]{2,1,0:T(8,128)(2,1)S(1)} %copy-done.4), kind=kOutput, calls=%fused_computation.121 | convolution fusion | flops 2532309760 | bytes 13109760 | tf_op jit(solution)/shard_map/dot_general | solution.py:44
  68.5 31.9 %all-gather.4.cloned.1.call-done = bf16[768,1280]{1,0:T(8,128)(2,1)} async-done(((bf16[192,1280]{1,0:T(8,128)(2,1)}), bf16[768,1280]{1,0:T(8,128)(2,1)}) %all-gather.4.cloned.1.call-update) | async-done | bytes 1966096 | tf_op jit(solution)/shard_map/all_gather | solution.py:68
  100.3 6.6 %convolution_convert_fusion.1 = bf16[1280,1280]{1,0:T(8,128)(2,1)} fusion(bf16[768,1280]{1,0:T(8,128)(2,1)} %all-gather.4.cloned.1.call-done, bf16[768,1280]{1,0:T(8,128)(2,1)} %get-tuple-element.30), kind=kOutput, calls=%fused_computation.1 | convolution fusion | flops 2518220800 | bytes 7208960 | tf_op jit(solution)/shard_map/dot_general | solution.py:67
  106.9 0.0 all-reduce.3.cloned.1.call-update
  106.9 0.2 reduce-scatter.2.cloned.1.call-start
  107.2 6.6 %convolution_convert_fusion.2 = bf16[768,1280]{1,0:T(8,128)(2,1)} fusion(bf16[768,1280]{1,0:T(8,128)(2,1)} %get-tuple-element.30, bf16[1280,1280]{1,0:T(8,128)(2,1)} %param.9), kind=kOutput, calls=%fused_computation.44 | convolution fusion | flops 2517565440 | bytes 7208960 | tf_op jit(solution)/shard_map/dot_general | solution.py:56
  113.8 0.0 reduce-scatter.2.cloned.1.call-update
  113.8 14.3 %psum.30 = bf16[1280]{0:T(1024)(128)(2,1)S(1)} all-reduce(bf16[1280]{0:T(1024)(128)(2,1)S(1)} %get-tuple-element.29), channel_id=1, replica_groups=mesh['dp'=8,'tp'=4] {'dp'}, use_global_device_ids=true, to_apply=%region_4.0 | all-reduce | flops 1280 | bytes 5120 | tf_op jit(solution)/shard_map/psum | solution.py:87
  128.1 0.6 convert_element_type.123
  128.7 84.3 %all-reduce.3.cloned.1.call-done = (bf16[1280,1280]{1,0:T(8,128)(2,1)}, bf16[1280,1280]{1,0:T(8,128)(2,1)}) async-done(((bf16[1280,1280]{1,0:T(8,128)(2,1)}, bf16[1280,1280]{1,0:T(8,128)(2,1)}), (bf16[1280,1280]{1,0:T(8,128)(2,1)}, bf16[1280,1280]{1,0:T(8,128)(2,1)})) %all-reduce.3.cloned.1.call-update) | async-done | bytes 6553616 | tf_op jit(solution)/shard_map/psum | solution.py:85
  213.1 0.0 copy-start.2
  213.1 5.4 %convert_element_type.119 = f32[1280,1280]{1,0:T(8,128)} convert(bf16[1280,1280]{1,0:T(8,128)(2,1)} %get-tuple-element.22) | non-fusion elementwise | flops 1638400 | bytes 9830400 | tf_op jit(solution)/shard_map/convert_element_type | solution.py:85
  218.4 0.0 copy-done.2
  218.4 3.3 %convert_element_type.122 = f32[1280,1280]{1,0:T(8,128)} convert(bf16[1280,1280]{1,0:T(8,128)(2,1)S(1)} %copy-done.2) | non-fusion elementwise | flops 1638400 | bytes 9830400 | tf_op jit(solution)/shard_map/convert_element_type | solution.py:86
  221.7 35.3 %reduce-scatter.2.cloned.1.call-done = bf16[192,1280]{1,0:T(8,128)(2,1)} async-done(((bf16[768,1280]{1,0:T(8,128)(2,1)}), bf16[192,1280]{1,0:T(8,128)(2,1)}) %reduce-scatter.2.cloned.1.call-update) | async-done | bytes 491536 | tf_op jit(solution)/shard_map/reduce_scatter | solution.py:55
  257.0 3.8 %fusion.66 = (f32[1280]{0:T(1024)S(1)}, f32[1280]{0:T(1024)S(1)}, f32[1280]{0:T(1024)S(1)}, f32[1280]{0:T(1024)S(1)}, f32[1280]{0:T(1024)S(1)}, /*index=5*/f32[1...) fusion(bf16[3,1280]{1,0:T(4,128)(2,1)S(1)} %collective-permute-done.3, bf16[192,1280]{1,0:T(8,128)(2,1)} %bitcast.132, ...), kind=kLoop, calls=%fused_computation.86 | loop fusion | flops 10804480 | bytes 2508800 | tf_op jit(solution)/shard_map/reduce_sum | solution.py:81
  260.8 0.0 copy-start.3
  260.9 0.7 copy-done.3
  261.6 1.3 collective-permute-start
  262.9 4.5 %collective-permute-start.1 = (bf16[3,1280]{1,0:T(4,128)(2,1)S(1)}, bf16[3,1280]{1,0:T(4,128)(2,1)S(1)}, u32[]{:S(2)}, u32[]{:S(2)}) collective-permute-start(bf16[3,1280]{1,0:T(4,128)(2,1)S(1)} %get-tuple-element.26), channel_id=1, source_target_pairs={{0,1},{1,2},{2,3},{4,5},{5,6},{6,7},{8,9},{9,10},{10,11},{12,13},{... | collective-permute-start | bytes 23048 | tf_op jit(solution)/shard_map/ppermute | solution.py:17
  267.4 0.1 stack.31
  267.5 40.2 %psum.31 = f32[7,1280]{1,0:T(8,128)} all-reduce(f32[7,1280]{1,0:T(8,128)S(1)} %stack.31), channel_id=1, replica_groups=mesh['dp'=8,'tp'=4] {'dp','tp'}, use_global_device_ids=true, to_apply=%region_12.0 | all-reduce | flops 8960 | bytes 71680 | tf_op jit(solution)/shard_map/psum | solution.py:83
  307.6 0.0 collective-permute-done
  307.6 0.0 collective-permute-done.1
  307.6 4.3 %fusion.76 = bf16[1,192,1280]{2,1,0:T(8,128)(2,1)} fusion(bf16[192,1280]{1,0:T(8,128)(2,1)} %copy-done.3, bf16[3,1280]{1,0:T(4,128)(2,1)S(1)} %collective-permute-done.1, f32[1280]{0:T(1024)S(1)} %get-tuple-element.20, f32[1280]{0:T(1024)S(1)} %get-tuple-element.21, f32[1280]{0:T(1024)S(1)} %get-tuple-element.16, f32[1280]{0:T(1024)S(1)} %get-tuple-element.17, ...), kind=kLoop, calls=%fused_computation.109 | loop fusion | flops 9830400 | bytes 1034240 | tf_op jit(solution)/shard_map/broadcast_in_dim | solution.py:89
  (8 shorter events, 0.0 us)
Async XLA Ops:
  7.2 56.6 %copy-start = (bf16[1280,1280]{1,0:T(8,128)(2,1)S(1)}, bf16[1280,1280]{1,0:T(8,128)(2,1)}, u32[]{:S(2)}) copy-start(bf16[1280,1280]{1,0:T(8,128)(2,1)} %param.10) | copy-start | bytes 9830404
  7.2 48.6 %all-gather.6.cloned.1.call-start = ((), (), s32[]{:S(2)}) async-start(), calls=%async_computation.3 | async-start | bytes 2457600 | tf_op jit(solution)/shard_map/all_gather | solution.py:42
  7.9 92.4 %all-gather.4.cloned.1.call-start = ((), (), s32[]{:S(2)}) async-start(), calls=%async_computation.2 | async-start | bytes 2457600 | tf_op jit(solution)/shard_map/all_gather | solution.py:68
  8.9 7.5 %collective-permute-start.2 = (bf16[3,1280]{1,0:T(4,128)(2,1)S(1)}, bf16[3,1280]{1,0:T(4,128)(2,1)S(1)}, u32[]{:S(2)}, u32[]{:S(2)}) collective-permute-start(bf16[3,1280]{1,0:T(4,128)(2,1)S(1)} %get-tuple-element.27), channel_id=1, source_target_pairs={{0,1},{1,2},{2,3},{4,5},{5,6},{6,7},{8,9},{9,10},{10,11},{12,13},{... | collective-permute-start | bytes 23048 | tf_op jit(solution)/shard_map/ppermute | solution.py:17
  13.9 5.6 %collective-permute-start.3 = (bf16[3,1280]{1,0:T(4,128)(2,1)S(1)}, bf16[3,1280]{1,0:T(4,128)(2,1)S(1)}, u32[]{:S(2)}, u32[]{:S(2)}) collective-permute-start(bf16[3,1280]{1,0:T(4,128)(2,1)S(1)} %get-tuple-element.28), channel_id=1, source_target_pairs={{1,0},{2,1},{3,2},{5,4},{6,5},{7,6},{9,8},{10,9},{11,10},{13,12},{... | collective-permute-start | bytes 23048 | tf_op jit(solution)/shard_map/ppermute | solution.py:19
  23.9 189.2 %all-reduce.3.cloned.1.call-start = ((), (), s32[]{:S(2)}) async-start(), calls=%async_computation.4 | async-start | bytes 13107200 | tf_op jit(solution)/shard_map/psum | solution.py:85
  55.8 7.9 %copy-start.1 = (f32[768,1280]{1,0:T(8,128)S(1)}, f32[768,1280]{1,0:T(8,128)}, u32[]{:S(2)}) copy-start(f32[768,1280]{1,0:T(8,128)} %fusion.38) | copy-start | bytes 11796484
  55.8 7.9 %copy-start.4 = (bf16[1,768,1280]{2,1,0:T(8,128)(2,1)S(1)}, bf16[1,768,1280]{2,1,0:T(8,128)(2,1)}, u32[]{:S(2)}) copy-start(bf16[1,768,1280]{2,1,0:T(8,128)(2,1)} %param.7) | copy-start | bytes 5898244
  55.8 7.9 %copy-start.5 = (bf16[1,768,1280]{2,1,0:T(8,128)(2,1)S(1)}, bf16[1,768,1280]{2,1,0:T(8,128)(2,1)}, u32[]{:S(2)}) copy-start(bf16[1,768,1280]{2,1,0:T(8,128)(2,1)} %all-gather.6.cloned.1.call-done) | copy-start | bytes 5898244
  106.9 150.0 %reduce-scatter.2.cloned.1.call-start = ((), (), s32[]{:S(2)}) async-start(), calls=%async_computation.1 | async-start | bytes 2457600 | tf_op jit(solution)/shard_map/reduce_scatter | solution.py:55
  213.1 5.4 %copy-start.2 = (bf16[1280,1280]{1,0:T(8,128)(2,1)S(1)}, bf16[1280,1280]{1,0:T(8,128)(2,1)}, u32[]{:S(2)}) copy-start(bf16[1280,1280]{1,0:T(8,128)(2,1)} %get-tuple-element.23) | copy-start | bytes 9830404
  260.8 0.8 copy-start.3
  261.6 46.1 %collective-permute-start = (bf16[3,1280]{1,0:T(4,128)(2,1)S(1)}, bf16[3,1280]{1,0:T(4,128)(2,1)S(1)}, u32[]{:S(2)}, u32[]{:S(2)}) collective-permute-start(bf16[3,1280]{1,0:T(4,128)(2,1)S(1)} %get-tuple-element.25), channel_id=1, source_target_pairs={{1,0},{2,1},{3,2},{5,4},{6,5},{7,6},{9,8},{10,9},{11,10},{13,12},{... | collective-permute-start | bytes 23048 | tf_op jit(solution)/shard_map/ppermute | solution.py:19
  262.9 44.8 %collective-permute-start.1 = (bf16[3,1280]{1,0:T(4,128)(2,1)S(1)}, bf16[3,1280]{1,0:T(4,128)(2,1)S(1)}, u32[]{:S(2)}, u32[]{:S(2)}) collective-permute-start(bf16[3,1280]{1,0:T(4,128)(2,1)S(1)} %get-tuple-element.26), channel_id=1, source_target_pairs={{0,1},{1,2},{2,3},{4,5},{5,6},{6,7},{8,9},{9,10},{10,11},{12,13},{... | collective-permute-start | bytes 23048 | tf_op jit(solution)/shard_map/ppermute | solution.py:17
Sparse Core Ops, SparseCore 0:
  9.6 46.2 all-gather.5
  58.0 42.3 all-gather.3
  107.1 105.9 all-reduce.2
  215.2 41.6 reduce-scatter.1
where the time goes:
time: 319 us; the launch traced here: 318 us
  waiting for transfers between devices  177 us (55%)
  blocking collectives  54.5 us (17%)
  other arithmetic  31.8 us (10%)
  matrix products  25.8 us (8%)
  between operations  13.9 us (4%)
  starting transfers between devices  12.4 us (4%)
    psum x1, waiting for transfers between devices, shards(): lax.psum(grad_w_in.astype(jnp.bfloat16), 'dp').astype(jnp.float32)  84.3 us
    psum x1, blocking collectives, shards(): grad_kernel = lax.psum(grad_kernel, ('dp', 'tp'))  40.2 us
    reduce_scatter x1, waiting for transfers between devices, shards(): lax.psum_scatter(lax.dot_general(buffer, w_in, (((1,), (1,)), ((), ())),...  35.3 us
    all_gather x1, waiting for transfers between devices, shards(): lax.all_gather(mixed, 'tp', axis=0, tiled=True)  31.9 us
    all_gather x1, waiting for transfers between devices, shards(): piece = lax.all_gather(grad_out, 'tp', axis=0, tiled=True)  21.8 us
    psum x1, blocking collectives, shards(): lax.psum(grad_bias.astype(jnp.bfloat16), 'dp').astype(jnp.float32)  14.3 us
    another operation x1, other arithmetic, gelu_exact(): return jax.nn.gelu(value, approximate=False)  10.1 us
    ppermute x2, starting transfers between devices, with_halo(): lax.ppermute(tail, axis, [(i, (i + 1) % count) for i in range(ends)])  9.5 us
  transfers between devices with their start and end apart: 8, of which 5 were waited for; matrix products, arithmetic and copies ran while one was open for 14% of the time, Pallas kernels for 0%

commit v1 on v0

--- a/solution.py
+++ b/solution.py
@@ -39,7 +39,13 @@
     hidden = saved_hidden[0]
     grad_out = upstream[0]
     length = tokens.shape[0]
-    piece = lax.all_gather(grad_out, "tp", axis=0, tiled=True)
+    peers = lax.axis_size("tp")
+    held, blocks = (grad_out, [grad_out])
+    for _ in range(peers - 1):
+        held = lax.ppermute(held, "tp", [(i_2, (i_2 + 1) % peers) for i_2 in range(peers)])
+        blocks.insert(0, held)
+    line = jnp.concatenate(blocks, axis=0)
+    piece = jnp.roll(line, (lax.axis_index("tp") + 1) * grad_out.shape[0], axis=0)
     hidden_rows = hidden.astype(jnp.float32)
     back_rows = lax.dot_general(
         piece, w_out, (((1,), (1,)), ((), ())), preferred_element_type=jnp.float32

time: 319 us -> 257 us (0.81)
  waiting for transfers between devices: 177 us -> 108 us
  local copies, waits for them, and re-layouts: 3.03 us -> 10.5 us
  matrix products: 25.8 us -> 22.3 us
    psum x1, waiting for transfers between devices: 84.3 us -> 54.8 us  [shards(): lax.psum(grad_w_in.astype(jnp.bfloat16), 'dp').astype(jnp.float32)]
    all_gather x1 -> x0, waiting for transfers between devices: 21.8 us -> none  [shards(): piece = lax.all_gather(grad_out, 'tp', axis=0, tiled=True)]
    ppermute x0 -> x3, waiting for transfers between devices: none -> 21.4 us  [shards(): lax.ppermute(held, 'tp', [(i_2, (i_2 + 1) % peers) for i_2 in range(peers)])]
    all_gather x1, waiting for transfers between devices: 31.9 us -> 10.9 us  [shards(): lax.all_gather(mixed, 'tp', axis=0, tiled=True)]
    reduce_scatter x1, waiting for transfers between devices: 35.3 us -> 21.3 us  [shards(): lax.psum_scatter(lax.dot_general(buffer, w_in, (((1,), (1,)), ((), ())),...]
    unnamed x12 -> x27, local copies, waits for them, and re-layouts: 0.7 us -> 9.51 us
  transfers between devices with their start and end apart: 8 -> 10, of which waited for: 5 -> 6; matrix products, arithmetic and copies ran while one was open for 14% -> 21% of each run, Pallas kernels for 0% -> 0%
where the time goes in v1:
time: 257 us
  waiting for transfers between devices  108 us (42%)
  blocking collectives  55.3 us (22%)
  other arithmetic  32.2 us (13%)
  matrix products  22.3 us (9%)
  starting transfers between devices  14 us (5%)
  between operations  14 us (5%)
  local copies, waits for them, and re-layouts  10.5 us (4%)
    psum x1, waiting for transfers between devices, shards(): lax.psum(grad_w_in.astype(jnp.bfloat16), 'dp').astype(jnp.float32)  54.8 us
    psum x1, blocking collectives, shards(): grad_kernel = lax.psum(grad_kernel, ('dp', 'tp'))  41.1 us
    ppermute x3, waiting for transfers between devices, shards(): lax.ppermute(held, 'tp', [(i_2, (i_2 + 1) % peers) for i_2 in range(peers)])  21.4 us
    reduce_scatter x1, waiting for transfers between devices, shards(): lax.psum_scatter(lax.dot_general(buffer, w_in, (((1,), (1,)), ((), ())),...  21.3 us
    psum x1, blocking collectives, shards(): lax.psum(grad_bias.astype(jnp.bfloat16), 'dp').astype(jnp.float32)  14.2 us
    all_gather x1, waiting for transfers between devices, shards(): lax.all_gather(mixed, 'tp', axis=0, tiled=True)  10.9 us
    another operation x1, other arithmetic, gelu_exact(): return jax.nn.gelu(value, approximate=False)  10.1 us
    unnamed x27, local copies, waits for them, and re-layouts  9.51 us
  transfers between devices with their start and end apart: 10, of which 6 were waited for; matrix products, arithmetic and copies ran while one was open for 21% of the time, Pallas kernels for 0%

profile of v1, /device:TPU:0, one launch (start us, length us, event | category | flops | bytes accessed | tf_op | source)
XLA Modules:
  0.0 256.8 jit_solution(11554418461380868126)
XLA Ops:
  7.2 0.0 copy-start
  7.2 0.0 copy-start.7
  7.2 0.0 all-gather.2.cloned.1.call-start
  7.2 3.1 %collective-permute-start = (bf16[192,1280]{1,0:T(8,128)(2,1)}, bf16[192,1280]{1,0:T(8,128)(2,1)}, u32[]{:S(2)}, u32[]{:S(2)}) collective-permute-start(bf16[192,1280]{1,0:T(8,128)(2,1)} %bitcast.125), channel_id=1, source_target_pairs={{0,1},{1,2},{2,3},{3,0},{4,5},{5,6},{6,7},{7,4},{8,9},{9,10},{10,1... | collective-permute-start | bytes 1474568 | tf_op jit(solution)/shard_map/ppermute | solution.py:45
  10.3 0.8 slice_bitcast_fusion.1
  11.1 3.5 %collective-permute-start.5 = (bf16[3,1280]{1,0:T(4,128)(2,1)S(1)}, bf16[3,1280]{1,0:T(4,128)(2,1)S(1)}, u32[]{:S(2)}, u32[]{:S(2)}) collective-permute-start(bf16[3,1280]{1,0:T(4,128)(2,1)S(1)} %get-tuple-element.27), channel_id=1, source_target_pairs={{0,1},{1,2},{2,3},{4,5},{5,6},{6,7},{8,9},{9,10},{10,11},{12,13},{... | collective-permute-start | bytes 23048 | tf_op jit(solution)/shard_map/ppermute | solution.py:17
  14.6 1.3 collective-permute-start.6
  15.9 8.2 %collective-permute-done = bf16[192,1280]{1,0:T(8,128)(2,1)} collective-permute-done((bf16[192,1280]{1,0:T(8,128)(2,1)}, bf16[192,1280]{1,0:T(8,128)(2,1)}, u32[]{:S(2)}, u32[]{:S(2)}) %collective-permute-start) | collective-permute-done | bytes 491552 | tf_op jit(solution)/shard_map/ppermute | solution.py:45
  24.1 0.0 collective-permute-start.1
  24.1 10.1 %fusion.38 = f32[768,1280]{1,0:T(8,128)} fusion(bf16[1,768,1280]{2,1,0:T(8,128)(2,1)} %param.7), kind=kLoop, calls=%fused_computation.43 | loop fusion | flops 61931520 | bytes 5898240 | tf_op jit(solution)/shard_map/jvp()/erfc | solution.py:27
  34.1 0.0 copy-done.7
  34.1 0.1 slice_reduce_fusion.6
  34.3 4.2 %collective-permute-done.1 = bf16[192,1280]{1,0:T(8,128)(2,1)} collective-permute-done((bf16[192,1280]{1,0:T(8,128)(2,1)}, bf16[192,1280]{1,0:T(8,128)(2,1)}, u32[]{:S(2)}, u32[]{:S(2)}) %collective-permute-start.1) | collective-permute-done | bytes 491552 | tf_op jit(solution)/shard_map/ppermute | solution.py:45
  38.5 0.0 collective-permute-start.2
  38.5 0.0 collective-permute-done.5
  38.5 0.0 collective-permute-done.6
  38.5 4.4 %fusion.52 = bf16[192,1280]{1,0:T(8,128)(2,1)} fusion(bf16[192,1280]{1,0:T(8,128)(2,1)} %bitcast.123, bf16[3,1280]{1,0:T(4,128)(2,1)S(1)} %collective-permute-done.6, bf16[3,1280]{1,0:T(4,128)(2,1)S(1)} %collective-permute-done.5, f32[1280]{0:T(1024)S(1)} %get-tuple-element.20, f32[1280]{0:T(1024)S(1)} %get-tuple-element.21, f32[1280]{0:T(1024)S(1)} %get-tuple-element.16, ...), kind=kLoop, calls=%fused_computation.72 | loop fusion | flops 9830400 | bytes 1034240 | tf_op jit(solution)/shard_map/convert_element_type | solution.py:34
  42.8 0.0 all-gather.2.cloned.1.call-update
  42.9 0.0 reduce-scatter.2.cloned.1.call-start
  42.9 0.0 copy-start.1
  42.9 0.0 copy-start.2
  42.9 0.0 copy-start.5
  43.0 9.0 %collective-permute-done.2 = bf16[192,1280]{1,0:T(8,128)(2,1)} collective-permute-done((bf16[192,1280]{1,0:T(8,128)(2,1)}, bf16[192,1280]{1,0:T(8,128)(2,1)}, u32[]{:S(2)}, u32[]{:S(2)}) %collective-permute-start.2) | collective-permute-done | bytes 491552 | tf_op jit(solution)/shard_map/ppermute | solution.py:45
  52.0 1.1 constant_dynamic-update-slice_fusion.7
  53.1 1.1 constant_dynamic-update-slice_fusion.6
  54.1 1.1 constant_dynamic-update-slice_fusion.5
  55.2 1.1 constant_dynamic-update-slice_fusion.4
  56.3 1.1 constant_dynamic-update-slice_fusion.3
  57.3 1.1 constant_dynamic-update-slice_fusion.2
  58.4 1.1 constant_dynamic-update-slice_fusion.1
  59.5 0.0 copy-done.1
  59.5 0.0 copy-done
  59.5 0.0 copy-done.2
  59.5 0.0 copy-done.5
  59.6 0.0 copy-start.6
  59.6 0.0 copy-start.8
  59.6 3.9 %fusion.80 = (bf16[1280]{0:T(1024)(128)(2,1)S(1)}, bf16[768,1280]{1,0:T(8,128)(2,1)S(1)}) fusion(f32[768,1280]{1,0:T(8,128)S(1)} %copy-done.2, bf16[1280,1280]{1,0:T(8,128)(2,1)S(1)} %copy-done, bf16[1536,1280]{1,0:T(8,128)(2,1)S(1)} %constant_dynamic-update-slice_fusion, s32[]{:T(128)S(6)} %select_n.14, bf16[1,768,1280]{2,1,0:T(8,128)(2,1)S(1)} %copy-done.5), kind=kOutput, calls=%fused_computation.130 | convolution fusion | flops 2532309760 | bytes 13109764 | tf_op jit(solution)/shard_map/dot_general | solution.py:50
  63.5 0.0 copy-done.6
  63.5 0.0 copy-start.9
  63.5 1.3 copy-done.9
  64.8 0.0 copy-done.8
  64.8 3.9 %convolution_convert_fusion.2 = bf16[768,1280]{1,0:T(8,128)(2,1)} fusion(bf16[768,1280]{1,0:T(8,128)(2,1)S(1)} %get-tuple-element.30, bf16[1280,1280]{1,0:T(8,128)(2,1)S(1)} %copy-done.8), kind=kOutput, calls=%fused_computation.44 | convolution fusion | flops 2517565440 | bytes 7208960 | tf_op jit(solution)/shard_map/dot_general | solution.py:62
  68.7 0.0 reduce-scatter.2.cloned.1.call-update
  68.8 0.2 all-reduce.3.cloned.1.call-start
  69.0 7.9 %convolution_convert_fusion = bf16[1280,1280]{1,0:T(8,128)(2,1)} fusion(f32[768,1280]{1,0:T(8,128)} %fusion.38, bf16[1,768,1280]{2,1,0:T(8,128)(2,1)} %param.7, bf16[1536,1280]{1,0:T(8,128)(2,1)} %copy-done.6, s32[]{:T(128)S(6)} %select_n.14), kind=kOutput, calls=%fused_computation | convolution fusion | flops 2522152960 | bytes 11141124 | tf_op jit(solution)/shard_map/dot_general | solution.py:56
  76.9 10.9 %all-gather.2.cloned.1.call-done = bf16[768,1280]{1,0:T(8,128)(2,1)} async-done(((bf16[192,1280]{1,0:T(8,128)(2,1)}), bf16[768,1280]{1,0:T(8,128)(2,1)}) %all-gather.2.cloned.1.call-update) | async-done | bytes 1966096 | tf_op jit(solution)/shard_map/all_gather | solution.py:74
  87.8 6.6 %convolution_convert_fusion.1 = bf16[1280,1280]{1,0:T(8,128)(2,1)} fusion(bf16[768,1280]{1,0:T(8,128)(2,1)} %all-gather.2.cloned.1.call-done, bf16[768,1280]{1,0:T(8,128)(2,1)} %copy-done.9), kind=kOutput, calls=%fused_computation.1 | convolution fusion | flops 2518220800 | bytes 7208960 | tf_op jit(solution)/shard_map/dot_general | solution.py:73
  94.4 0.0 all-reduce.3.cloned.1.call-update
  94.4 14.2 %psum.30 = bf16[1280]{0:T(1024)(128)(2,1)S(1)} all-reduce(bf16[1280]{0:T(1024)(128)(2,1)S(1)} %get-tuple-element.29), channel_id=1, replica_groups=mesh['dp'=8,'tp'=4] {'dp'}, use_global_device_ids=true, to_apply=%region_4.5 | all-reduce | flops 1280 | bytes 5120 | tf_op jit(solution)/shard_map/psum | solution.py:93
  108.6 0.6 convert_element_type.123
  109.2 21.3 %reduce-scatter.2.cloned.1.call-done = bf16[192,1280]{1,0:T(8,128)(2,1)} async-done(((bf16[768,1280]{1,0:T(8,128)(2,1)}), bf16[192,1280]{1,0:T(8,128)(2,1)}) %reduce-scatter.2.cloned.1.call-update) | async-done | bytes 491536 | tf_op jit(solution)/shard_map/reduce_scatter | solution.py:61
  130.5 3.8 %fusion.66 = (f32[1280]{0:T(1024)S(1)}, f32[1280]{0:T(1024)S(1)}, f32[1280]{0:T(1024)S(1)}, f32[1280]{0:T(1024)S(1)}, f32[1280]{0:T(1024)S(1)}, /*index=5*/f32[1...) fusion(bf16[3,1280]{1,0:T(4,128)(2,1)S(1)} %collective-permute-done.6, bf16[192,1280]{1,0:T(8,128)(2,1)} %bitcast.124, ...), kind=kLoop, calls=%fused_computation.86 | loop fusion | flops 10804480 | bytes 2508800 | tf_op jit(solution)/shard_map/reduce_sum | solution.py:87
  134.3 0.0 copy-start.4
  134.4 0.7 copy-done.4
  135.1 1.3 collective-permute-start.3
  136.4 4.5 %collective-permute-start.4 = (bf16[3,1280]{1,0:T(4,128)(2,1)S(1)}, bf16[3,1280]{1,0:T(4,128)(2,1)S(1)}, u32[]{:S(2)}, u32[]{:S(2)}) collective-permute-start(bf16[3,1280]{1,0:T(4,128)(2,1)S(1)} %get-tuple-element.26), channel_id=1, source_target_pairs={{0,1},{1,2},{2,3},{4,5},{5,6},{6,7},{8,9},{9,10},{10,11},{12,13},{... | collective-permute-start | bytes 23048 | tf_op jit(solution)/shard_map/ppermute | solution.py:17
  141.0 0.1 stack.31
  141.0 41.1 %psum.31 = f32[7,1280]{1,0:T(8,128)} all-reduce(f32[7,1280]{1,0:T(8,128)S(1)} %stack.31), channel_id=1, replica_groups=mesh['dp'=8,'tp'=4] {'dp','tp'}, use_global_device_ids=true, to_apply=%region_12.13 | all-reduce | flops 8960 | bytes 71680 | tf_op jit(solution)/shard_map/psum | solution.py:89
  182.1 0.0 collective-permute-done.3
  182.1 0.0 collective-permute-done.4
  182.1 4.7 %fusion.75 = bf16[1,192,1280]{2,1,0:T(8,128)(2,1)} fusion(bf16[192,1280]{1,0:T(8,128)(2,1)} %copy-done.4, bf16[3,1280]{1,0:T(4,128)(2,1)S(1)} %collective-permute-done.4, f32[1280]{0:T(1024)S(1)} %get-tuple-element.20, f32[1280]{0:T(1024)S(1)} %get-tuple-element.21, f32[1280]{0:T(1024)S(1)} %get-tuple-element.16, f32[1280]{0:T(1024)S(1)} %get-tuple-element.17, ...), kind=kLoop, calls=%fused_computation.108 | loop fusion | flops 9830400 | bytes 1034240 | tf_op jit(solution)/shard_map/broadcast_in_dim | solution.py:95
  186.8 54.8 %all-reduce.3.cloned.1.call-done = (bf16[1280,1280]{1,0:T(8,128)(2,1)}, bf16[1280,1280]{1,0:T(8,128)(2,1)}) async-done(((bf16[1280,1280]{1,0:T(8,128)(2,1)}, bf16[1280,1280]{1,0:T(8,128)(2,1)}), (bf16[1280,1280]{1,0:T(8,128)(2,1)}, bf16[1280,1280]{1,0:T(8,128)(2,1)})) %all-reduce.3.cloned.1.call-update) | async-done | bytes 6553616 | tf_op jit(solution)/shard_map/psum | solution.py:91
  241.6 5.4 %convert_element_type.119 = f32[1280,1280]{1,0:T(8,128)} convert(bf16[1280,1280]{1,0:T(8,128)(2,1)} %get-tuple-element.22) | non-fusion elementwise | flops 1638400 | bytes 9830400 | tf_op jit(solution)/shard_map/convert_element_type | solution.py:91
  247.0 3.3 %convert_element_type.122 = f32[1280,1280]{1,0:T(8,128)} convert(bf16[1280,1280]{1,0:T(8,128)(2,1)S(1)} %copy-done.3) | non-fusion elementwise | flops 1638400 | bytes 9830400 | tf_op jit(solution)/shard_map/convert_element_type | solution.py:92
  (11 shorter events, 0.1 us)
Async XLA Ops:
  7.2 52.4 %copy-start = (bf16[1280,1280]{1,0:T(8,128)(2,1)S(1)}, bf16[1280,1280]{1,0:T(8,128)(2,1)}, u32[]{:S(2)}) copy-start(bf16[1280,1280]{1,0:T(8,128)(2,1)} %param.10) | copy-start | bytes 9830404
  7.2 27.0 %copy-start.7 = (f32[7,1280]{1,0:T(8,128)S(1)}, f32[7,1280]{1,0:T(8,128)}, u32[]{:S(2)}) copy-start(f32[7,1280]{1,0:T(8,128)} %param.11) | copy-start | bytes 107524
  7.2 80.6 %all-gather.2.cloned.1.call-start = ((), (), s32[]{:S(2)}) async-start(), calls=%async_computation.2 | async-start | bytes 2457600 | tf_op jit(solution)/shard_map/all_gather | solution.py:74
  7.2 16.8 %collective-permute-start = (bf16[192,1280]{1,0:T(8,128)(2,1)}, bf16[192,1280]{1,0:T(8,128)(2,1)}, u32[]{:S(2)}, u32[]{:S(2)}) collective-permute-start(bf16[192,1280]{1,0:T(8,128)(2,1)} %bitcast.125), channel_id=1, source_target_pairs={{0,1},{1,2},{2,3},{3,0},{4,5},{5,6},{6,7},{7,4},{8,9},{9,10},{10,1... | collective-permute-start | bytes 1474568 | tf_op jit(solution)/shard_map/ppermute | solution.py:45
  11.1 27.4 %collective-permute-start.5 = (bf16[3,1280]{1,0:T(4,128)(2,1)S(1)}, bf16[3,1280]{1,0:T(4,128)(2,1)S(1)}, u32[]{:S(2)}, u32[]{:S(2)}) collective-permute-start(bf16[3,1280]{1,0:T(4,128)(2,1)S(1)} %get-tuple-element.27), channel_id=1, source_target_pairs={{0,1},{1,2},{2,3},{4,5},{5,6},{6,7},{8,9},{9,10},{10,11},{12,13},{... | collective-permute-start | bytes 23048 | tf_op jit(solution)/shard_map/ppermute | solution.py:17
  14.6 23.9 %collective-permute-start.6 = (bf16[3,1280]{1,0:T(4,128)(2,1)S(1)}, bf16[3,1280]{1,0:T(4,128)(2,1)S(1)}, u32[]{:S(2)}, u32[]{:S(2)}) collective-permute-start(bf16[3,1280]{1,0:T(4,128)(2,1)S(1)} %get-tuple-element.28), channel_id=1, source_target_pairs={{1,0},{2,1},{3,2},{5,4},{6,5},{7,6},{9,8},{10,9},{11,10},{13,12},{... | collective-permute-start | bytes 23048 | tf_op jit(solution)/shard_map/ppermute | solution.py:19
  24.1 14.4 %collective-permute-start.1 = (bf16[192,1280]{1,0:T(8,128)(2,1)}, bf16[192,1280]{1,0:T(8,128)(2,1)}, u32[]{:S(2)}, u32[]{:S(2)}) collective-permute-start(bf16[192,1280]{1,0:T(8,128)(2,1)} %collective-permute-done), channel_id=1, source_target_pairs={{0,1},{1,2},{2,3},{3,0},{4,5},{5,6},{6,7},{7,4},{8,9},{9,10},{10,1... | collective-permute-start | bytes 1474568 | tf_op jit(solution)/shard_map/ppermute | solution.py:45
  38.5 13.5 %collective-permute-start.2 = (bf16[192,1280]{1,0:T(8,128)(2,1)}, bf16[192,1280]{1,0:T(8,128)(2,1)}, u32[]{:S(2)}, u32[]{:S(2)}) collective-permute-start(bf16[192,1280]{1,0:T(8,128)(2,1)} %collective-permute-done.1), channel_id=1, source_target_pairs={{0,1},{1,2},{2,3},{3,0},{4,5},{5,6},{6,7},{7,4},{8,9},{9,10},{10,1... | collective-permute-start | bytes 1474568 | tf_op jit(solution)/shard_map/ppermute | solution.py:45
  42.9 87.7 %reduce-scatter.2.cloned.1.call-start = ((), (), s32[]{:S(2)}) async-start(), calls=%async_computation.1 | async-start | bytes 2457600 | tf_op jit(solution)/shard_map/reduce_scatter | solution.py:61
  42.9 16.6 %copy-start.1 = (bf16[1,192,1280]{2,1,0:T(8,128)(2,1)S(1)}, bf16[1,192,1280]{2,1,0:T(8,128)(2,1)}, u32[]{:S(2)}) copy-start(bf16[1,192,1280]{2,1,0:T(8,128)(2,1)} %param.8) | copy-start | bytes 1474564
  42.9 16.6 %copy-start.2 = (f32[768,1280]{1,0:T(8,128)S(1)}, f32[768,1280]{1,0:T(8,128)}, u32[]{:S(2)}) copy-start(f32[768,1280]{1,0:T(8,128)} %fusion.38) | copy-start | bytes 11796484
  42.9 16.6 %copy-start.5 = (bf16[1,768,1280]{2,1,0:T(8,128)(2,1)S(1)}, bf16[1,768,1280]{2,1,0:T(8,128)(2,1)}, u32[]{:S(2)}) copy-start(bf16[1,768,1280]{2,1,0:T(8,128)(2,1)} %param.7) | copy-start | bytes 5898244
  59.6 3.9 %copy-start.6 = (bf16[1536,1280]{1,0:T(8,128)(2,1)}, bf16[1536,1280]{1,0:T(8,128)(2,1)S(1)}, u32[]{:S(2)}) copy-start(bf16[1536,1280]{1,0:T(8,128)(2,1)S(1)} %constant_dynamic-update-slice_fusion) | copy-start | bytes 11796484
  59.6 5.2 %copy-start.8 = (bf16[1280,1280]{1,0:T(8,128)(2,1)S(1)}, bf16[1280,1280]{1,0:T(8,128)(2,1)}, u32[]{:S(2)}) copy-start(bf16[1280,1280]{1,0:T(8,128)(2,1)} %param.9) | copy-start | bytes 9830404
  63.5 1.3 copy-start.9
  68.8 172.8 %all-reduce.3.cloned.1.call-start = ((), (), s32[]{:S(2)}) async-start(), calls=%async_computation.3 | async-start | bytes 13107200 | tf_op jit(solution)/shard_map/psum | solution.py:91
  134.3 0.8 copy-start.4
  135.1 47.0 %collective-permute-start.3 = (bf16[3,1280]{1,0:T(4,128)(2,1)S(1)}, bf16[3,1280]{1,0:T(4,128)(2,1)S(1)}, u32[]{:S(2)}, u32[]{:S(2)}) collective-permute-start(bf16[3,1280]{1,0:T(4,128)(2,1)S(1)} %get-tuple-element.25), channel_id=1, source_target_pairs={{1,0},{2,1},{3,2},{5,4},{6,5},{7,6},{9,8},{10,9},{11,10},{13,12},{... | collective-permute-start | bytes 23048 | tf_op jit(solution)/shard_map/ppermute | solution.py:19
  136.4 45.7 %collective-permute-start.4 = (bf16[3,1280]{1,0:T(4,128)(2,1)S(1)}, bf16[3,1280]{1,0:T(4,128)(2,1)S(1)}, u32[]{:S(2)}, u32[]{:S(2)}) collective-permute-start(bf16[3,1280]{1,0:T(4,128)(2,1)S(1)} %get-tuple-element.26), channel_id=1, source_target_pairs={{0,1},{1,2},{2,3},{4,5},{5,6},{6,7},{8,9},{9,10},{10,11},{12,13},{... | collective-permute-start | bytes 23048 | tf_op jit(solution)/shard_map/ppermute | solution.py:17
  241.6 5.4 %copy-start.3 = (bf16[1280,1280]{1,0:T(8,128)(2,1)S(1)}, bf16[1280,1280]{1,0:T(8,128)(2,1)}, u32[]{:S(2)}) copy-start(bf16[1280,1280]{1,0:T(8,128)(2,1)} %get-tuple-element.23) | copy-start | bytes 9830404
Sparse Core Ops, SparseCore 0:
  43.0 44.7 all-gather.1
  90.1 40.4 reduce-scatter.1
  134.5 107.0 all-reduce.2
